TPU v7x, 32 devices: a whole 2x2x4 slice. The times are simulated.
32 devices in a mesh: face: 8 (over z, core), sub: 4 (over y, x).
Axes of the slice: x: 2, y: 2, z: 4, core: 2. Of those that a mesh axis runs over, the one named last changes fastest.
Arguments:
- mesh_latent: bfloat16 [8192, 512], P(('face', 'sub')), may hold values from -6 to 6
- edge_latent: bfloat16 [65536, 512], P(('face', 'sub')), may hold values from -6 to 6
- grid_features: bfloat16 [8192, 384], P(('face', 'sub')), may hold values from -6 to 6
- senders: int32 [65536], P(('face', 'sub')), may hold values from 0 to 383, as said below
- receivers: int32 [65536], P(('face', 'sub')), may hold values from 0 to 255
- send_lists: int32 [32, 4, 32], P(('face', 'sub')), may hold values from -1 to 255, as said below
- link_sources: int32 [16384], P(('face', 'sub')), may hold values from 0 to 255
- link_targets: int32 [16384], P(('face', 'sub')), may hold values from 0 to 255
- node_area: float32 [8192], P(('face', 'sub')), may hold values from 0.25 to 4.5
- grid_weight: bfloat16 [384, 512], P(None, 'sub'), may hold values from -0.3125 to 0.3125
- encode_weight: bfloat16 [1024, 512], P('sub'), may hold values from -0.1875 to 0.1875
- edge_first: bfloat16 [1, 1536, 512], P(None, 'sub'), may hold values from -0.15625 to 0.15625
- edge_second: bfloat16 [1, 512, 512], P(None, 'sub'), may hold values from -0.25 to 0.25
- node_first: bfloat16 [1, 1024, 512], P(None, 'sub'), may hold values from -0.1875 to 0.1875
- node_second: bfloat16 [1, 512, 512], P(None, 'sub'), may hold values from -0.25 to 0.25
Outputs:
- mesh_result: bfloat16 [8192, 512], P(('face', 'sub'))
- edge_result: bfloat16 [65536, 512], P(('face', 'sub'))
- masses: float32 [1, 512], replicated
Inputs may be any that keep to these rules, and one draw needn't show every extreme that they name: `send_lists`: entries are the sending partition's own node numbers, or -1 for an unused slot; in every list the used slots come first, hold distinct nodes and number 32 // 2 or more; for every list number some partition uses all 32 slots. `senders`: A value below 256 names one of the partition's own nodes; 256 + d * 32 + k names slot k of the list with number d that the partition receives, and that slot is always a used one.
All inputs are finite; a program needn't handle non-finite values.
Results may differ from a plain program's by a relative error of at most 0.008.
Values may be sent and summed in bfloat16 or wider, within the bound.
A program may use at most 64 MiB of HBM per device.

v0:
```python
import jax
import jax.numpy as jnp
from jax import lax
from jax.sharding import PartitionSpec as P


def passed_along(value, axis, steps):
    count = lax.axis_size(axis)
    pairs = [(source, (source + steps) % count) for source in range(count)]
    return lax.ppermute(value, axis, pairs)


def fold_rows(weight, operand):
    return jnp.dot(
        operand,
        lax.all_gather(weight, "sub", axis=0, tiled=True),
        preferred_element_type=jnp.float32,
    )


def edge_rows(weight, operand):
    storage = jnp.zeros((1, weight.shape[1]), jnp.bfloat16)
    total = jnp.dot(
        operand,
        lax.all_gather(weight, "sub", axis=0, tiled=True),
        preferred_element_type=jnp.float32,
    )
    return (total, storage)


def along_face(values, offset):
    return passed_along(values, "face", offset)


def along_sub(values, offset):
    return passed_along(values, "sub", offset)


def per_device(
    mesh_latent,
    edge_latent,
    grid_features,
    senders,
    receivers,
    send_lists,
    link_sources,
    link_targets,
    node_area,
    grid_weight,
    encode_weight,
    edge_first,
    edge_second,
    node_first,
    node_second,
):
    node_rows = mesh_latent.shape[0]
    nodes_all = node_rows * lax.axis_size("face") * lax.axis_size("sub")
    grid_latent = jax.nn.silu(
        jnp.dot(
            grid_features,
            lax.all_gather(grid_weight, "sub", axis=1, tiled=True),
            preferred_element_type=jnp.float32,
        )
    ).astype(jnp.bfloat16)

    def project(weight, operand):
        return fold_rows(weight, operand)

    node_ids = jnp.arange(node_rows, dtype=jnp.int32)
    joined = jnp.concatenate(
        [jnp.take(grid_latent, link_sources, axis=0), jnp.take(mesh_latent, link_targets, axis=0)],
        axis=1,
    )
    messages = jax.nn.silu(project(encode_weight, joined)).astype(jnp.bfloat16)
    target_onehot = (link_targets[:, None] == node_ids[None, :]).astype(jnp.bfloat16)
    arriving = lax.dot_general(
        target_onehot, messages, (((0,), (0,)), ((), ())), preferred_element_type=jnp.float32
    )
    latent = (mesh_latent.astype(jnp.float32) + arriving).astype(jnp.bfloat16)
    halo_lists = send_lists[0]
    list_mask = (halo_lists >= 0)[:, :, None]
    receive_onehot = (receivers[:, None] == node_ids[None, :]).astype(jnp.bfloat16)
    edge_state = edge_latent
    picked = jnp.take(latent, jnp.maximum(halo_lists, 0), axis=0)
    picked = jnp.where(list_mask, picked, jnp.zeros((), jnp.bfloat16))
    lower_face = along_face(picked[0], 1)
    upper_face = along_face(picked[1], -1)
    lower_sub = along_sub(picked[2], 1)
    upper_sub = along_sub(picked[3], -1)
    arrived = jnp.concatenate([lower_face, upper_face, lower_sub, upper_sub], axis=0)
    receiving_rows = jnp.take(latent, receivers, axis=0)
    node_table = jnp.concatenate([latent, arrived], axis=0)
    inputs = jnp.concatenate(
        [edge_state, jnp.take(node_table, senders, axis=0), receiving_rows], axis=1
    )
    before, unused_rows = edge_rows(edge_first[0], inputs)
    hidden = jax.nn.silu(before).astype(jnp.bfloat16)
    edge_state = (edge_state.astype(jnp.float32) + project(edge_second[0], hidden)).astype(
        jnp.bfloat16
    )
    incoming = lax.dot_general(
        receive_onehot, edge_state, (((0,), (0,)), ((), ())), preferred_element_type=jnp.float32
    ).astype(jnp.bfloat16)
    node_hidden = jax.nn.silu(
        project(node_first[0], jnp.concatenate([latent, incoming], axis=1))
    ).astype(jnp.bfloat16)
    latent = (latent.astype(jnp.float32) + project(node_second[0], node_hidden)).astype(
        jnp.bfloat16
    )
    totals = [jnp.dot(node_area, latent.astype(jnp.float32), precision=lax.Precision.HIGHEST)]
    stacked = lax.psum(jnp.stack(totals), ("face", "sub"))
    masses = stacked / nodes_all
    return (latent, edge_state, masses)


def solution(mesh):
    in_specs = (
        P(("face", "sub"), None),
        P(("face", "sub"), None),
        P(("face", "sub"), None),
        P(("face", "sub")),
        P(("face", "sub")),
        P(("face", "sub"), None, None),
        P(("face", "sub")),
        P(("face", "sub")),
        P(("face", "sub")),
        P(None, "sub"),
        P("sub", None),
        P(None, "sub", None),
        P(None, "sub", None),
        P(None, "sub", None),
        P(None, "sub", None),
    )
    out_specs = (P(("face", "sub"), None), P(("face", "sub"), None), P())
    return jax.shard_map(
        per_device, mesh=mesh, in_specs=in_specs, out_specs=out_specs, check_vma=False
    )
```

profile of v0, /device:TPU:0, one launch (start us, length us, event | category | flops | bytes accessed | tf_op | source)
XLA Modules:
  0.0 153.9 jit_solution(15797503033091889898)
XLA Ops:
  13.5 0.7 fusion.46
  14.2 1.3 compare_and_fusion.1
  15.5 0.7 fusion.47
  16.2 1.3 compare_and_fusion
  17.5 12.5 %all_gather.18 = bf16[384,512]{1,0:T(8,128)(2,1)S(1)} all-gather(bf16[384,128]{1,0:T(8,128)(2,1)} %param.26), channel_id=1, replica_groups=mesh['face'=8,'sub'=4] {'sub'}, dimensions={1}, use_global_device_ids=true | all-gather | bytes 491520 | tf_op jit(solution)/shard_map/all_gather | solution.py:61
  30.1 13.3 %all-gather.1 = bf16[1,512,512]{2,1,0:T(8,128)(2,1)} all-gather(bf16[1,128,512]{2,1,0:T(8,128)(2,1)} %param.29), channel_id=3, replica_groups=mesh['face'=8,'sub'=4] {'sub'}, dimensions={1}, use_global_device_ids=true | all-gather | bytes 655360 | tf_op jit(solution)/shard_map/all_gather | solution.py:16
  43.5 10.7 %all-gather.3 = bf16[1,512,512]{2,1,0:T(8,128)(2,1)S(1)} all-gather(bf16[1,128,512]{2,1,0:T(8,128)(2,1)S(1)} %copy-done.3), channel_id=5, replica_groups=mesh['face'=8,'sub'=4] {'sub'}, dimensions={1}, use_global_device_ids=true | all-gather | bytes 655360 | tf_op jit(solution)/shard_map/all_gather | solution.py:16
  54.6 2.0 %gather_fusion.3 = bf16[512,512]{1,0:T(8,128)(2,1)S(1)} fusion(bf16[256,512]{1,0:T(8,128)(2,1)S(1)} %multiply_convert_fusion.4, s32[1024]{0:T(1024)S(1)} %pad_clamp_fusion.2), kind=kCustom, calls=%fused_computation.clone | custom fusion | bytes 1050624 | tf_op jit(solution)/shard_map/jit(_take)/gather | solution.py:71
  56.6 2.0 %gather_fusion.4 = bf16[512,512]{1,0:T(8,128)(2,1)S(1)} fusion(bf16[256,512]{1,0:T(8,128)(2,1)S(1)} %copy-done.1, s32[1024]{0:T(1024)S(1)} %pad_clamp_fusion.1), kind=kCustom, calls=%fused_computation.1.clone | custom fusion | bytes 1050624 | tf_op jit(solution)/shard_map/jit(_take)/gather | solution.py:71
  59.2 2.3 %constant_dynamic-update-slice_fusion.4 = (bf16[384,512]{1,0:T(8,128)(2,1)S(1)}, bf16[256,512]{1,0:T(8,128)(2,1)S(1)}) fusion(bf16[1024,512]{1,0:T(8,128)(2,1)} %all-gather.8.cloned.1.call-done, bf16[512,512]{1,0:T(8,128)(2,1)S(1)} %get-tuple-element.12, bf16[512,512]{1,0:T(8,128)(2,1)S(1)} %get-tuple-element.13, s32[512]{0:T(512)S(1)} %copy-done.6, ...), kind=kOutput, calls=%fused_computation.55 | convolution fusion | flops 675020800 | bytes 2885632 | tf_op jit(solution)/shard_map/dot_general | solution.py:76
  61.5 0.8 gather_fusion
  63.1 3.5 %collective-permute-start.1 = (bf16[32,512]{1,0:T(8,128)(2,1)}, bf16[32,512]{1,0:T(8,128)(2,1)}, u32[]{:S(2)}, u32[]{:S(2)}) collective-permute-start(bf16[32,512]{1,0:T(8,128)(2,1)} %get-tuple-element.6), channel_id=1, source_target_pairs={{0,28},{4,0},{8,4},{12,8},{16,12},{20,16},{24,20},{28,24},{1,29},{... | collective-permute-start | bytes 98312 | tf_op jit(solution)/shard_map/ppermute | solution.py:10
  67.1 2.5 %collective-permute-start.3 = (bf16[32,512]{1,0:T(8,128)(2,1)}, bf16[32,512]{1,0:T(8,128)(2,1)S(1)}, u32[]{:S(2)}, u32[]{:S(2)}) collective-permute-start(bf16[32,512]{1,0:T(8,128)(2,1)} %get-tuple-element.4), channel_id=1, source_target_pairs={{0,3},{1,0},{2,1},{3,2},{4,7},{5,4},{6,5},{7,6},{8,11},{9,8},{10,9... | collective-permute-start | bytes 98312 | tf_op jit(solution)/shard_map/ppermute | solution.py:10
  69.6 7.5 %gather_fusion.2 = bf16[2048,512]{1,0:T(8,128)(2,1)S(1)} fusion(bf16[256,512]{1,0:T(8,128)(2,1)S(1)} %get-tuple-element.11, s32[2048]{0:T(1024)S(1)} %fusion.47), kind=kCustom, calls=%fused_computation.4 | custom fusion | bytes 4202496 | tf_op jit(solution)/shard_map/jit(_take)/gather | solution.py:91
  77.1 2.2 %broadcast_select_fusion = bf16[2048,512]{1,0:T(8,128)(2,1)} fusion(bf16[2048,512]{1,0:T(8,128)(2,1)S(1)} %gather_fusion.2, pred[2048]{0:T(1024)(128)(4,1)} %compare_and_fusion), kind=kLoop, calls=%fused_computation.14 | loop fusion | flops 1048576 | bytes 4196352 | tf_op jit(solution)/shard_map/jit(_take)/select_n | solution.py:91
  79.4 0.8 constant_dynamic-update-slice_fusion.3
  80.1 0.8 constant_dynamic-update-slice_fusion.2
  80.9 7.5 %gather_fusion.1 = bf16[2048,512]{1,0:T(8,128)(2,1)S(1)} fusion(bf16[384,512]{1,0:T(8,128)(2,1)S(1)} %constant_dynamic-update-slice_fusion, s32[2048]{0:T(1024)S(1)} %fusion.46), kind=kCustom, calls=%fused_computation.3 | custom fusion | bytes 4202496 | tf_op jit(solution)/shard_map/jit(_take)/gather | solution.py:94
  88.5 1.6 %broadcast_select_fusion.1 = bf16[2048,512]{1,0:T(8,128)(2,1)} fusion(bf16[2048,512]{1,0:T(8,128)(2,1)S(1)} %gather_fusion.1, pred[2048]{0:T(1024)(128)(4,1)S(1)} %copy-done.5), kind=kLoop, calls=%fused_computation.15 | loop fusion | flops 1048576 | bytes 4196352 | tf_op jit(solution)/shard_map/jit(_take)/select_n | solution.py:94
  90.0 8.5 %add_convert_fusion = bf16[2048,512]{1,0:T(8,128)(2,1)S(1)} fusion(bf16[2048,512]{1,0:T(8,128)(2,1)} %param.18, bf16[2048,512]{1,0:T(8,128)(2,1)} %broadcast_select_fusion, bf16[2048,512]{1,0:T(8,128)(2,1)} %broadcast_select_fusion.1, bf16[1,1536,512]{2,1,0:T(8,128)(2,1)} %all-gather.10.cloned.1.call-done, bf16[1,512,512]{2,1,0:T(8,128)(2,1)} %all-gather.1), kind=kOutput, calls=%fused_computation.11 | convolution fusion | flops 4322230272 | bytes 10485760 | tf_op jit(solution)/shard_map/dot_general | solution.py:14
  98.6 1.8 %fusion.8 = bf16[256,512]{1,0:T(8,128)(2,1)} fusion(bf16[2048,512]{1,0:T(8,128)(2,1)S(1)} %add_convert_fusion, s32[2048]{0:T(1024)S(1)} %copy-done.4), kind=kOutput, calls=%fused_computation.20 | convolution fusion | flops 537526272 | bytes 2367488 | tf_op jit(solution)/shard_map/dot_general | solution.py:101
  100.4 4.8 %all-gather.12.cloned.1.call-done = bf16[1,1024,512]{2,1,0:T(8,128)(2,1)} async-done(((bf16[1,256,512]{2,1,0:T(8,128)(2,1)}), bf16[1,1024,512]{2,1,0:T(8,128)(2,1)}) %all-gather.12.cloned.1.call-update) | async-done | bytes 1048592 | tf_op jit(solution)/shard_map/all_gather | solution.py:16
  105.3 2.0 %fusion.10 = bf16[256,512]{1,0:T(8,128)(2,1)S(1)} fusion(bf16[1,512,512]{2,1,0:T(8,128)(2,1)S(1)} %all-gather.3, bf16[1,1024,512]{2,1,0:T(8,128)(2,1)} %all-gather.12.cloned.1.call-done, bf16[256,512]{1,0:T(8,128)(2,1)} %fusion.8, bf16[256,512]{1,0:T(8,128)(2,1)S(1)} %get-tuple-element.11), kind=kOutput, calls=%fused_computation.22 | convolution fusion | flops 404750336 | bytes 2359296 | tf_op jit(solution)/shard_map/dot_general | solution.py:14
  107.5 39.2 %psum.7 = f32[1,512]{1,0:T(1,128)S(1)} all-reduce(f32[1,512]{1,0:T(1,128)S(1)} %fusion.59), channel_id=1, replica_groups=mesh['face'=8,'sub'=4] {'face','sub'}, use_global_device_ids=true, to_apply=%region_0.2 | all-reduce | flops 512 | bytes 4096 | tf_op jit(solution)/shard_map/psum | solution.py:111
  (50 shorter events, 9.4 us)
Async XLA Ops:
  7.2 47.0 %copy-start = (bf16[256,384]{1,0:T(8,128)(2,1)S(1)}, bf16[256,384]{1,0:T(8,128)(2,1)}, u32[]{:S(2)}) copy-start(bf16[256,384]{1,0:T(8,128)(2,1)} %param.19) | copy-start | bytes 589828
  7.2 36.3 %copy-start.3 = (bf16[1,128,512]{2,1,0:T(8,128)(2,1)S(1)}, bf16[1,128,512]{2,1,0:T(8,128)(2,1)}, u32[]{:S(2)}) copy-start(bf16[1,128,512]{2,1,0:T(8,128)(2,1)} %param.31) | copy-start | bytes 393220
  7.2 51.6 %all-gather.8.cloned.1.call-start = ((), (), s32[]{:S(2)}) async-start(), calls=%async_computation | async-start | bytes 1310720 | tf_op jit(solution)/shard_map/all_gather | solution.py:16
  7.9 82.1 %all-gather.10.cloned.1.call-start = ((), (), s32[]{:S(2)}) async-start(), calls=%async_computation.1 | async-start | bytes 1966080 | tf_op jit(solution)/shard_map/all_gather | solution.py:25
  8.7 96.6 %all-gather.12.cloned.1.call-start = ((), (), s32[]{:S(2)}) async-start(), calls=%async_computation.2 | async-start | bytes 1310720 | tf_op jit(solution)/shard_map/all_gather | solution.py:16
  54.6 2.0 %copy-start.1 = (bf16[256,512]{1,0:T(8,128)(2,1)S(1)}, bf16[256,512]{1,0:T(8,128)(2,1)}, u32[]{:S(2)}) copy-start(bf16[256,512]{1,0:T(8,128)(2,1)} %param.17) | copy-start | bytes 786436
  58.5 0.7 copy-start.6
  63.1 16.2 %collective-permute-start = (bf16[32,512]{1,0:T(8,128)(2,1)}, bf16[32,512]{1,0:T(8,128)(2,1)}, u32[]{:S(2)}, u32[]{:S(2)}) collective-permute-start(bf16[32,512]{1,0:T(8,128)(2,1)} %get-tuple-element.7), channel_id=1, source_target_pairs={{0,4},{4,8},{8,12},{12,16},{16,20},{20,24},{24,28},{28,0},{1,5},{5... | collective-permute-start | bytes 98312 | tf_op jit(solution)/shard_map/ppermute | solution.py:10
  63.1 17.0 %collective-permute-start.1 = (bf16[32,512]{1,0:T(8,128)(2,1)}, bf16[32,512]{1,0:T(8,128)(2,1)}, u32[]{:S(2)}, u32[]{:S(2)}) collective-permute-start(bf16[32,512]{1,0:T(8,128)(2,1)} %get-tuple-element.6), channel_id=1, source_target_pairs={{0,28},{4,0},{8,4},{12,8},{16,12},{20,16},{24,20},{28,24},{1,29},{... | collective-permute-start | bytes 98312 | tf_op jit(solution)/shard_map/ppermute | solution.py:10
  66.7 14.2 %collective-permute-start.2 = (bf16[32,512]{1,0:T(8,128)(2,1)}, bf16[32,512]{1,0:T(8,128)(2,1)S(1)}, u32[]{:S(2)}, u32[]{:S(2)}) collective-permute-start(bf16[32,512]{1,0:T(8,128)(2,1)} %get-tuple-element.5), channel_id=1, source_target_pairs={{0,1},{1,2},{2,3},{3,0},{4,5},{5,6},{6,7},{7,4},{8,9},{9,10},{10,1... | collective-permute-start | bytes 98312 | tf_op jit(solution)/shard_map/ppermute | solution.py:10
  67.1 13.8 %collective-permute-start.3 = (bf16[32,512]{1,0:T(8,128)(2,1)}, bf16[32,512]{1,0:T(8,128)(2,1)S(1)}, u32[]{:S(2)}, u32[]{:S(2)}) collective-permute-start(bf16[32,512]{1,0:T(8,128)(2,1)} %get-tuple-element.4), channel_id=1, source_target_pairs={{0,3},{1,0},{2,1},{3,2},{4,7},{5,4},{6,5},{7,6},{8,11},{9,8},{10,9... | collective-permute-start | bytes 98312 | tf_op jit(solution)/shard_map/ppermute | solution.py:10
  80.9 7.6 %copy-start.5 = (pred[2048]{0:T(1024)(128)(4,1)S(1)}, pred[2048]{0:T(1024)(128)(4,1)}, u32[]{:S(2)}) copy-start(pred[2048]{0:T(1024)(128)(4,1)} %compare_and_fusion.1) | copy-start | bytes 6148
  90.0 8.5 %copy-start.4 = (s32[2048]{0:T(1024)S(1)}, s32[2048]{0:T(1024)}, u32[]{:S(2)}) copy-start(s32[2048]{0:T(1024)} %param.21) | copy-start | bytes 24580
  98.6 8.7 %copy-start.8 = (bf16[2048,512]{1,0:T(8,128)(2,1)}, bf16[2048,512]{1,0:T(8,128)(2,1)S(1)}, u32[]{:S(2)}) copy-start(bf16[2048,512]{1,0:T(8,128)(2,1)S(1)} %add_convert_fusion) | copy-start | bytes 6291460
  100.4 6.9 %copy-start.7 = (f32[256]{0:T(256)S(1)}, f32[256]{0:T(256)}, u32[]{:S(2)}) copy-start(f32[256]{0:T(256)} %param.25) | copy-start | bytes 3076
  107.3 40.1 %copy-start.2 = (bf16[256,512]{1,0:T(8,128)(2,1)}, bf16[256,512]{1,0:T(8,128)(2,1)S(1)}, u32[]{:S(2)}) copy-start(bf16[256,512]{1,0:T(8,128)(2,1)S(1)} %fusion.10) | copy-start | bytes 786436
Sparse Core Ops, SparseCore 0:
  9.8 32.7 all-gather.7
  44.4 32.7 all-gather.9
  79.1 26.1 all-gather.11
where the time goes:
time: 155 us; the launch traced here: 154 us
  blocking collectives  75.8 us (49%)
  local copies, waits for them, and re-layouts  22.6 us (15%)
  matrix products  15.3 us (10%)
  between operations  14 us (9%)
  other arithmetic  12.7 us (8%)
  waiting for transfers between devices  6.92 us (4%)
  starting transfers between devices  6.58 us (4%)
    psum x1, blocking collectives, per_device(): stacked = lax.psum(jnp.stack(totals), ('face', 'sub'))  39.2 us
    all_gather x2, blocking collectives, fold_rows(): lax.all_gather(weight, 'sub', axis=0, tiled=True)  24 us
    all_gather x1, blocking collectives, per_device(): lax.all_gather(grid_weight, 'sub', axis=1, tiled=True)  12.5 us
    dot_general x2, matrix products, fold_rows(): jnp.dot(operand, lax.all_gather(weight, 'sub', axis=0, tiled=True), prefe...  10.5 us
    gather x1, local copies, waits for them, and re-layouts, per_device(): jnp.take(node_table, senders, axis=0)  7.54 us
    gather x1, local copies, waits for them, and re-layouts, per_device(): receiving_rows = jnp.take(latent, receivers, axis=0)  7.53 us
    ppermute x4, starting transfers between devices, passed_along(): return lax.ppermute(value, axis, pairs)  6.47 us
    all_gather x2, waiting for transfers between devices, fold_rows(): lax.all_gather(weight, 'sub', axis=0, tiled=True)  4.85 us
  transfers between devices with their start and end apart: 7, of which 1 were waited for; matrix products, arithmetic and copies ran while one was open for 31% of the time, Pallas kernels for 0%

commit v1 on v0

--- a/solution.py
+++ b/solution.py
@@ -108,7 +108,9 @@
         jnp.bfloat16
     )
     totals = [jnp.dot(node_area, latent.astype(jnp.float32), precision=lax.Precision.HIGHEST)]
-    stacked = lax.psum(jnp.stack(totals), ("face", "sub"))
+    part = jnp.stack(totals)
+    parts = lax.all_gather(part, ("face", "sub"))
+    stacked = jnp.sum(parts, axis=0)
     masses = stacked / nodes_all
     return (latent, edge_state, masses)
 

time: 155 us -> 183 us (1.18)
  blocking collectives: 75.8 us -> 104 us
    all_gather x0 -> x1, blocking collectives: none -> 67.1 us  [per_device(): parts = lax.all_gather(part, ('face', 'sub'))]
    psum x1 -> x0, blocking collectives: 39.2 us -> none  [per_device(): stacked = lax.psum(jnp.stack(totals), ('face', 'sub'))]
  transfers between devices with their start and end apart: 7 -> 7, of which waited for: 1 -> 1; matrix products, arithmetic and copies ran while one was open for 31% -> 26% of each run, Pallas kernels for 0% -> 0%
where the time goes in v1:
time: 183 us; the launch traced here: 182 us
  blocking collectives  104 us (57%)
  local copies, waits for them, and re-layouts  22.6 us (12%)
  matrix products  15.3 us (8%)
  between operations  14 us (8%)
  other arithmetic  12.8 us (7%)
  waiting for transfers between devices  6.92 us (4%)
  starting transfers between devices  6.58 us (4%)
    all_gather x1, blocking collectives, per_device(): parts = lax.all_gather(part, ('face', 'sub'))  67.1 us
    all_gather x2, blocking collectives, fold_rows(): lax.all_gather(weight, 'sub', axis=0, tiled=True)  24 us
    all_gather x1, blocking collectives, per_device(): lax.all_gather(grid_weight, 'sub', axis=1, tiled=True)  12.5 us
    dot_general x2, matrix products, fold_rows(): jnp.dot(operand, lax.all_gather(weight, 'sub', axis=0, tiled=True), prefe...  10.5 us
    gather x1, local copies, waits for them, and re-layouts, per_device(): jnp.take(node_table, senders, axis=0)  7.54 us
    gather x1, local copies, waits for them, and re-layouts, per_device(): receiving_rows = jnp.take(latent, receivers, axis=0)  7.53 us
    ppermute x4, starting transfers between devices, passed_along(): return lax.ppermute(value, axis, pairs)  6.47 us
    all_gather x2, waiting for transfers between devices, fold_rows(): lax.all_gather(weight, 'sub', axis=0, tiled=True)  4.85 us
  transfers between devices with their start and end apart: 7, of which 1 were waited for; matrix products, arithmetic and copies ran while one was open for 26% of the time, Pallas kernels for 0%

profile of v1, /device:TPU:0, one launch (start us, length us, event | category | flops | bytes accessed | tf_op | source)
XLA Modules:
  0.0 181.8 jit_solution(9777850057149666593)
XLA Ops:
  13.5 0.7 fusion.46
  14.2 1.3 compare_and_fusion.1
  15.5 0.7 fusion.47
  16.2 1.3 compare_and_fusion
  17.5 12.5 %all_gather.21 = bf16[384,512]{1,0:T(8,128)(2,1)S(1)} all-gather(bf16[384,128]{1,0:T(8,128)(2,1)} %param.26), channel_id=1, replica_groups=mesh['face'=8,'sub'=4] {'sub'}, dimensions={1}, use_global_device_ids=true | all-gather | bytes 491520 | tf_op jit(solution)/shard_map/all_gather | solution.py:61
  30.1 13.3 %all-gather.1 = bf16[1,512,512]{2,1,0:T(8,128)(2,1)} all-gather(bf16[1,128,512]{2,1,0:T(8,128)(2,1)} %param.29), channel_id=3, replica_groups=mesh['face'=8,'sub'=4] {'sub'}, dimensions={1}, use_global_device_ids=true | all-gather | bytes 655360 | tf_op jit(solution)/shard_map/all_gather | solution.py:16
  43.5 10.7 %all-gather.3 = bf16[1,512,512]{2,1,0:T(8,128)(2,1)S(1)} all-gather(bf16[1,128,512]{2,1,0:T(8,128)(2,1)S(1)} %copy-done.3), channel_id=5, replica_groups=mesh['face'=8,'sub'=4] {'sub'}, dimensions={1}, use_global_device_ids=true | all-gather | bytes 655360 | tf_op jit(solution)/shard_map/all_gather | solution.py:16
  54.6 2.0 %gather_fusion.3 = bf16[512,512]{1,0:T(8,128)(2,1)S(1)} fusion(bf16[256,512]{1,0:T(8,128)(2,1)S(1)} %multiply_convert_fusion.4, s32[1024]{0:T(1024)S(1)} %pad_clamp_fusion.2), kind=kCustom, calls=%fused_computation.clone | custom fusion | bytes 1050624 | tf_op jit(solution)/shard_map/jit(_take)/gather | solution.py:71
  56.6 2.0 %gather_fusion.4 = bf16[512,512]{1,0:T(8,128)(2,1)S(1)} fusion(bf16[256,512]{1,0:T(8,128)(2,1)S(1)} %copy-done.1, s32[1024]{0:T(1024)S(1)} %pad_clamp_fusion.1), kind=kCustom, calls=%fused_computation.1.clone | custom fusion | bytes 1050624 | tf_op jit(solution)/shard_map/jit(_take)/gather | solution.py:71
  59.2 2.3 %constant_dynamic-update-slice_fusion.4 = (bf16[384,512]{1,0:T(8,128)(2,1)S(1)}, bf16[256,512]{1,0:T(8,128)(2,1)S(1)}) fusion(bf16[1024,512]{1,0:T(8,128)(2,1)} %all-gather.10.cloned.1.call-done, bf16[512,512]{1,0:T(8,128)(2,1)S(1)} %get-tuple-element.12, bf16[512,512]{1,0:T(8,128)(2,1)S(1)} %get-tuple-element.13, s32[512]{0:T(512)S(1)} %copy-done.6, ...), kind=kOutput, calls=%fused_computation.56 | convolution fusion | flops 675020800 | bytes 2885632 | tf_op jit(solution)/shard_map/dot_general | solution.py:76
  61.5 0.8 gather_fusion
  63.1 3.5 %collective-permute-start.1 = (bf16[32,512]{1,0:T(8,128)(2,1)}, bf16[32,512]{1,0:T(8,128)(2,1)}, u32[]{:S(2)}, u32[]{:S(2)}) collective-permute-start(bf16[32,512]{1,0:T(8,128)(2,1)} %get-tuple-element.6), channel_id=1, source_target_pairs={{0,28},{4,0},{8,4},{12,8},{16,12},{20,16},{24,20},{28,24},{1,29},{... | collective-permute-start | bytes 98312 | tf_op jit(solution)/shard_map/ppermute | solution.py:10
  67.1 2.5 %collective-permute-start.3 = (bf16[32,512]{1,0:T(8,128)(2,1)}, bf16[32,512]{1,0:T(8,128)(2,1)S(1)}, u32[]{:S(2)}, u32[]{:S(2)}) collective-permute-start(bf16[32,512]{1,0:T(8,128)(2,1)} %get-tuple-element.4), channel_id=1, source_target_pairs={{0,3},{1,0},{2,1},{3,2},{4,7},{5,4},{6,5},{7,6},{8,11},{9,8},{10,9... | collective-permute-start | bytes 98312 | tf_op jit(solution)/shard_map/ppermute | solution.py:10
  69.6 7.5 %gather_fusion.2 = bf16[2048,512]{1,0:T(8,128)(2,1)S(1)} fusion(bf16[256,512]{1,0:T(8,128)(2,1)S(1)} %get-tuple-element.11, s32[2048]{0:T(1024)S(1)} %fusion.47), kind=kCustom, calls=%fused_computation.4 | custom fusion | bytes 4202496 | tf_op jit(solution)/shard_map/jit(_take)/gather | solution.py:91
  77.1 2.2 %broadcast_select_fusion = bf16[2048,512]{1,0:T(8,128)(2,1)} fusion(bf16[2048,512]{1,0:T(8,128)(2,1)S(1)} %gather_fusion.2, pred[2048]{0:T(1024)(128)(4,1)} %compare_and_fusion), kind=kLoop, calls=%fused_computation.14 | loop fusion | flops 1048576 | bytes 4196352 | tf_op jit(solution)/shard_map/jit(_take)/select_n | solution.py:91
  79.4 0.8 constant_dynamic-update-slice_fusion.3
  80.1 0.8 constant_dynamic-update-slice_fusion.2
  80.9 7.5 %gather_fusion.1 = bf16[2048,512]{1,0:T(8,128)(2,1)S(1)} fusion(bf16[384,512]{1,0:T(8,128)(2,1)S(1)} %constant_dynamic-update-slice_fusion, s32[2048]{0:T(1024)S(1)} %fusion.46), kind=kCustom, calls=%fused_computation.3 | custom fusion | bytes 4202496 | tf_op jit(solution)/shard_map/jit(_take)/gather | solution.py:94
  88.5 1.6 broadcast_select_fusion.1
  90.0 8.5 %add_convert_fusion = bf16[2048,512]{1,0:T(8,128)(2,1)S(1)} fusion(bf16[2048,512]{1,0:T(8,128)(2,1)} %param.18, bf16[2048,512]{1,0:T(8,128)(2,1)} %broadcast_select_fusion, bf16[2048,512]{1,0:T(8,128)(2,1)} %broadcast_select_fusion.1, bf16[1,1536,512]{2,1,0:T(8,128)(2,1)} %all-gather.12.cloned.1.call-done, bf16[1,512,512]{2,1,0:T(8,128)(2,1)} %all-gather.1), kind=kOutput, calls=%fused_computation.11 | convolution fusion | flops 4322230272 | bytes 10485760 | tf_op jit(solution)/shard_map/dot_general | solution.py:14
  98.6 1.8 %fusion.8 = bf16[256,512]{1,0:T(8,128)(2,1)} fusion(bf16[2048,512]{1,0:T(8,128)(2,1)S(1)} %add_convert_fusion, s32[2048]{0:T(1024)S(1)} %copy-done.4), kind=kOutput, calls=%fused_computation.20 | convolution fusion | flops 537526272 | bytes 2367488 | tf_op jit(solution)/shard_map/dot_general | solution.py:101
  100.4 4.8 %all-gather.14.cloned.1.call-done = bf16[1,1024,512]{2,1,0:T(8,128)(2,1)} async-done(((bf16[1,256,512]{2,1,0:T(8,128)(2,1)}), bf16[1,1024,512]{2,1,0:T(8,128)(2,1)}) %all-gather.14.cloned.1.call-update) | async-done | bytes 1048592 | tf_op jit(solution)/shard_map/all_gather | solution.py:16
  105.3 2.0 %fusion.10 = bf16[256,512]{1,0:T(8,128)(2,1)S(1)} fusion(bf16[1,512,512]{2,1,0:T(8,128)(2,1)S(1)} %all-gather.3, bf16[1,1024,512]{2,1,0:T(8,128)(2,1)} %all-gather.14.cloned.1.call-done, bf16[256,512]{1,0:T(8,128)(2,1)} %fusion.8, bf16[256,512]{1,0:T(8,128)(2,1)S(1)} %get-tuple-element.11), kind=kOutput, calls=%fused_computation.22 | convolution fusion | flops 404750336 | bytes 2359296 | tf_op jit(solution)/shard_map/dot_general | solution.py:14
  107.5 67.1 %all-gather.5 = f32[32,1,512]{2,1,0:T(1,128)S(1)} all-gather(f32[1,1,512]{2,1,0:T(1,128)S(1)} %convolution_bitcast_fusion), channel_id=6, replica_groups=mesh['face'=8,'sub'=4] {'face','sub'}, dimensions={0}, use_global_device_ids=true | all-gather | bytes 67584 | tf_op jit(solution)/shard_map/all_gather | solution.py:112
  (51 shorter events, 9.5 us)
Async XLA Ops:
  7.2 47.0 %copy-start = (bf16[256,384]{1,0:T(8,128)(2,1)S(1)}, bf16[256,384]{1,0:T(8,128)(2,1)}, u32[]{:S(2)}) copy-start(bf16[256,384]{1,0:T(8,128)(2,1)} %param.19) | copy-start | bytes 589828
  7.2 36.3 %copy-start.3 = (bf16[1,128,512]{2,1,0:T(8,128)(2,1)S(1)}, bf16[1,128,512]{2,1,0:T(8,128)(2,1)}, u32[]{:S(2)}) copy-start(bf16[1,128,512]{2,1,0:T(8,128)(2,1)} %param.31) | copy-start | bytes 393220
  7.2 51.6 %all-gather.10.cloned.1.call-start = ((), (), s32[]{:S(2)}) async-start(), calls=%async_computation | async-start | bytes 1310720 | tf_op jit(solution)/shard_map/all_gather | solution.py:16
  7.9 82.1 %all-gather.12.cloned.1.call-start = ((), (), s32[]{:S(2)}) async-start(), calls=%async_computation.1 | async-start | bytes 1966080 | tf_op jit(solution)/shard_map/all_gather | solution.py:25
  8.7 96.6 %all-gather.14.cloned.1.call-start = ((), (), s32[]{:S(2)}) async-start(), calls=%async_computation.2 | async-start | bytes 1310720 | tf_op jit(solution)/shard_map/all_gather | solution.py:16
  54.6 2.0 %copy-start.1 = (bf16[256,512]{1,0:T(8,128)(2,1)S(1)}, bf16[256,512]{1,0:T(8,128)(2,1)}, u32[]{:S(2)}) copy-start(bf16[256,512]{1,0:T(8,128)(2,1)} %param.17) | copy-start | bytes 786436
  58.5 0.7 copy-start.6
  63.1 16.2 %collective-permute-start = (bf16[32,512]{1,0:T(8,128)(2,1)}, bf16[32,512]{1,0:T(8,128)(2,1)}, u32[]{:S(2)}, u32[]{:S(2)}) collective-permute-start(bf16[32,512]{1,0:T(8,128)(2,1)} %get-tuple-element.7), channel_id=1, source_target_pairs={{0,4},{4,8},{8,12},{12,16},{16,20},{20,24},{24,28},{28,0},{1,5},{5... | collective-permute-start | bytes 98312 | tf_op jit(solution)/shard_map/ppermute | solution.py:10
  63.1 17.0 %collective-permute-start.1 = (bf16[32,512]{1,0:T(8,128)(2,1)}, bf16[32,512]{1,0:T(8,128)(2,1)}, u32[]{:S(2)}, u32[]{:S(2)}) collective-permute-start(bf16[32,512]{1,0:T(8,128)(2,1)} %get-tuple-element.6), channel_id=1, source_target_pairs={{0,28},{4,0},{8,4},{12,8},{16,12},{20,16},{24,20},{28,24},{1,29},{... | collective-permute-start | bytes 98312 | tf_op jit(solution)/shard_map/ppermute | solution.py:10
  66.7 14.2 %collective-permute-start.2 = (bf16[32,512]{1,0:T(8,128)(2,1)}, bf16[32,512]{1,0:T(8,128)(2,1)S(1)}, u32[]{:S(2)}, u32[]{:S(2)}) collective-permute-start(bf16[32,512]{1,0:T(8,128)(2,1)} %get-tuple-element.5), channel_id=1, source_target_pairs={{0,1},{1,2},{2,3},{3,0},{4,5},{5,6},{6,7},{7,4},{8,9},{9,10},{10,1... | collective-permute-start | bytes 98312 | tf_op jit(solution)/shard_map/ppermute | solution.py:10
  67.1 13.8 %collective-permute-start.3 = (bf16[32,512]{1,0:T(8,128)(2,1)}, bf16[32,512]{1,0:T(8,128)(2,1)S(1)}, u32[]{:S(2)}, u32[]{:S(2)}) collective-permute-start(bf16[32,512]{1,0:T(8,128)(2,1)} %get-tuple-element.4), channel_id=1, source_target_pairs={{0,3},{1,0},{2,1},{3,2},{4,7},{5,4},{6,5},{7,6},{8,11},{9,8},{10,9... | collective-permute-start | bytes 98312 | tf_op jit(solution)/shard_map/ppermute | solution.py:10
  80.9 7.6 %copy-start.5 = (pred[2048]{0:T(1024)(128)(4,1)S(1)}, pred[2048]{0:T(1024)(128)(4,1)}, u32[]{:S(2)}) copy-start(pred[2048]{0:T(1024)(128)(4,1)} %compare_and_fusion.1) | copy-start | bytes 6148
  90.0 8.5 %copy-start.4 = (s32[2048]{0:T(1024)S(1)}, s32[2048]{0:T(1024)}, u32[]{:S(2)}) copy-start(s32[2048]{0:T(1024)} %param.21) | copy-start | bytes 24580
  98.6 8.7 %copy-start.8 = (bf16[2048,512]{1,0:T(8,128)(2,1)}, bf16[2048,512]{1,0:T(8,128)(2,1)S(1)}, u32[]{:S(2)}) copy-start(bf16[2048,512]{1,0:T(8,128)(2,1)S(1)} %add_convert_fusion) | copy-start | bytes 6291460
  100.4 6.9 %copy-start.7 = (f32[256]{0:T(256)S(1)}, f32[256]{0:T(256)}, u32[]{:S(2)}) copy-start(f32[256]{0:T(256)} %param.25) | copy-start | bytes 3076
  107.3 68.0 %copy-start.2 = (bf16[256,512]{1,0:T(8,128)(2,1)}, bf16[256,512]{1,0:T(8,128)(2,1)S(1)}, u32[]{:S(2)}) copy-start(bf16[256,512]{1,0:T(8,128)(2,1)S(1)} %fusion.10) | copy-start | bytes 786436
Sparse Core Ops, SparseCore 0:
  9.8 32.7 all-gather.9
  44.4 32.7 all-gather.11
  79.1 26.1 all-gather.13
